TPU v7x, 128 devices: a whole 4x4x4 slice. The times are simulated.
128 devices in a mesh: row: 8 (over z_lo, x), col: 16 (over y, z_hi, core).
Axes of the slice: x: 4, y: 4, z: 4 (z_hi: 2, z_lo: 2; z = z_hi * 2 + z_lo), core: 2. Of those that a mesh axis runs over, the one named last changes fastest.
Arguments:
- gate_weight: bfloat16 [4608, 36864], P('row', 'col'), may hold values from -8.838835 to 8.838835
- up_weight: bfloat16 [4608, 36864], P('row', 'col'), may hold values from -8.838835 to 8.838835
- routes: int32 [2, 8], replicated, may hold values from 0 to 7, each once within a row
Outputs:
- gate_serving: bfloat16 [4608, 36864], P('col', 'row')
- up_serving: bfloat16 [4608, 36864], P('col', 'row')
- scales: float32 [2, 36864], P(None, 'row')
Inputs may be any that keep to these rules, and one draw needn't show every extreme that they name: Each row of routes names every serving rank's piece once.
All inputs are finite; a program needn't handle non-finite values. Where the computation divides by a largest or mean magnitude, that divisor is 1e-20 or more.
Results may differ from a plain program's by a relative error of at most 0.001.
Values may be sent and summed in bfloat16 or wider, within the bound.
No kernel may reach another device: no remote copies, remote signals or barrier semaphores. Data moves between devices by JAX's collectives and lax.ppermute only.
A program may use at most 64 MiB of HBM per device.

v0:
```python
import jax
import jax.numpy as jnp
from jax import lax
from jax.sharding import Mesh
from jax.sharding import PartitionSpec as P

COL = ("col_0", "col_1", "col_2")
EPSILON = 1e-06
LIMIT = 4.0


def copy_for_each(value, axis):
    devices = lax.axis_size(axis)
    return lax.all_to_all(
        jnp.broadcast_to(value[None], (devices, *value.shape)), axis, 0, 0, tiled=True
    )


def of_everyone(value, axis):
    everything = copy_for_each(value, axis)
    return jnp.max(everything, axis=0)


def in_one(arrays, axis):
    flat, at, outs = (jnp.concatenate([a.reshape(-1) for a in arrays]), 0, [])
    so_far = of_everyone(flat, axis)
    for a in arrays:
        outs.append(so_far[at : at + a.size].reshape(a.shape))
        at += a.size
    return tuple(outs)


def in_order(pieces, dim):
    pieces = jnp.moveaxis(pieces, 0, dim)
    lengths = pieces.shape
    return pieces.reshape(*lengths[:dim], lengths[dim] * lengths[dim + 1], *lengths[dim + 2 :])


def all_blocks(value, axes, order):
    pieces = value
    for k in order:
        pieces = lax.all_gather(pieces, axes[k])
    done = order[::-1]
    back = [done.index(k) for k in range(len(axes))]
    pieces = pieces.transpose(*back, *range(len(axes), pieces.ndim))
    return pieces.reshape(-1, *value.shape)


def gathered_by_axis(value, axes, order, dim):
    return in_order(all_blocks(value, axes, order), dim)


def column_peaks(weight):
    return jnp.max(jnp.abs(weight), axis=0).astype(jnp.float32)


def quantize(weight, peaks):
    factor = LIMIT / (peaks + EPSILON)
    return (weight.astype(jnp.float32) * factor[None, :]).astype(jnp.bfloat16)


def order_pieces(weight, order, pieces):
    height, width = weight.shape
    shaped = weight.reshape(height, pieces, width // pieces)
    return jnp.take(shaped, order, axis=1).reshape(height, width)


def own_piece(peaks, pick, pieces):
    shaped = ((peaks + EPSILON) / LIMIT).reshape(pieces, -1)
    return lax.dynamic_index_in_dim(shaped, pick, 0, keepdims=False)


def shards(gate_weight, up_weight, routes):
    pieces = lax.axis_size("row")
    row_index = lax.axis_index("row")
    gate_peaks, up_peaks = in_one((column_peaks(gate_weight), column_peaks(up_weight)), "row")
    gate_sent = order_pieces(quantize(gate_weight, gate_peaks), routes[0], pieces)
    up_sent = order_pieces(quantize(up_weight, up_peaks), routes[1], pieces)
    gate_serving, up_serving = (
        lax.all_to_all(
            lax.all_to_all(gate_sent, "row", split_axis=1, concat_axis=0, tiled=True),
            COL,
            split_axis=0,
            concat_axis=1,
            tiled=True,
        ),
        lax.all_to_all(
            lax.all_to_all(up_sent, "row", split_axis=1, concat_axis=0, tiled=True),
            COL,
            split_axis=0,
            concat_axis=1,
            tiled=True,
        ),
    )
    chosen = jnp.take(routes, row_index, axis=1)
    local_scales = jnp.stack(
        [own_piece(gate_peaks, chosen[0], pieces), own_piece(up_peaks, chosen[1], pieces)]
    )
    scales = gathered_by_axis(local_scales, COL, (1, 0, 2), 1)
    return (gate_serving, up_serving, scales)


def solution(mesh):
    finer = Mesh(
        mesh.devices.reshape(mesh.shape["row"], 4, 2, 2), ("row", "col_0", "col_1", "col_2")
    )
    return jax.shard_map(
        shards,
        mesh=finer,
        in_specs=(P("row", COL), P("row", COL), P()),
        out_specs=(P(COL, "row"), P(COL, "row"), P(None, "row")),
        check_vma=False,
    )
```

profile of v0, /device:TPU:1, one launch (start us, length us, event | category | flops | bytes accessed | tf_op | source)
XLA Modules:
  0.0 239.6 jit_solution(6475498258166576045)
XLA Ops:
  0.6 0.0 copy-start
  0.6 0.0 copy-start.2
  0.7 3.3 %abs_reduce_fusion = (bf16[2304]{0:T(1024)(128)(2,1)S(1)}, bf16[2304]{0:T(1024)(128)(2,1)S(1)}) fusion(bf16[576,2304]{1,0:T(8,128)(2,1)} %param.6, bf16[576,2304]{1,0:T(8,128)(2,1)} %param.5), kind=kLoop, calls=%fused_computation.6 | loop fusion | flops 5303808 | bytes 5317632 | tf_op jit(solution)/shard_map/reduce_max | solution.py:54
  3.9 0.7 broadcast_in_dim.25
  4.7 6.2 %all-to-all-start = ((f32[8,1,4608]{2,1,0:T(1,128)}), f32[8,1,4608]{2,1,0:T(1,128)S(1)}, u32[]{:S(2)}, u32[]{:S(2)}) async-start(f32[8,1,4608]{2,1,0:T(1,128)} %broadcast_in_dim.25), calls=%async_computation | async-start | bytes 294912 | tf_op jit(solution)/shard_map/all_to_all | solution.py:14
  10.9 0.0 copy-done.2
  10.9 0.0 copy-done
  10.9 3.0 %copy.45 = bf16[576,2304]{0,1:T(8,128)(2,1)} copy(bf16[576,2304]{1,0:T(8,128)(2,1)S(1)} %copy-done) | data formatting | bytes 5308416 | tf_op args[0]
  13.9 2.5 %all-to-all-done = f32[8,1,4608]{2,1,0:T(1,128)S(1)} async-done(((f32[8,1,4608]{2,1,0:T(1,128)}), f32[8,1,4608]{2,1,0:T(1,128)S(1)}, u32[]{:S(2)}, u32[]{:S(2)}) %all-to-all-start) | async-done | bytes 147488 | tf_op jit(solution)/shard_map/all_to_all | solution.py:14
  16.4 0.1 reduce_max.29
  16.5 0.6 fusion
  17.1 2.4 multiply_convert_fusion.1
  19.5 2.5 %gather_fusion = bf16[8,576,288]{1,2,0:T(8,128)(2,1)} fusion(bf16[576,8,288]{0,2,1:T(8,128)(2,1)S(1)} %bitcast.36, s32[1024]{0:T(1024)S(1)} %pad_clamp_fusion.1), kind=kCustom, calls=%fused_computation.clone | custom fusion | bytes 5308448 | tf_op jit(solution)/shard_map/jit(_take)/gather | solution.py:65
  22.1 3.8 %select_bitcast_fusion.1 = bf16[576,8,288]{0,2,1:T(8,128)(2,1)} fusion(bf16[8,576,288]{1,2,0:T(8,128)(2,1)} %gather_fusion, pred[8]{0:T(512)(128)(4,1)S(1)} %get-tuple-element.23), kind=kLoop, calls=%fused_computation.5 | loop fusion | flops 1327104 | bytes 5308424 | tf_op jit(solution)/shard_map/jit(_take)/select_n | solution.py:65
  25.9 0.0 copy-start.1
  25.9 4.7 %all-to-all-start.1 = ((bf16[576,8,288]{0,2,1:T(8,128)(2,1)}), bf16[576,8,288]{0,2,1:T(8,128)(2,1)}, u32[]{:S(2)}, u32[]{:S(2)}) async-start(bf16[576,8,288]{0,2,1:T(8,128)(2,1)} %select_bitcast_fusion.1), calls=%async_computation.1 | async-start | bytes 5898240 | tf_op jit(solution)/shard_map/all_to_all | solution.py:81
  30.6 0.0 copy-done.1
  30.6 3.0 %copy.50 = bf16[576,2304]{0,1:T(8,128)(2,1)} copy(bf16[576,2304]{1,0:T(8,128)(2,1)S(1)} %copy-done.1) | data formatting | bytes 5308416 | tf_op args[1]
  33.6 2.4 multiply_convert_fusion
  36.0 2.6 %gather_fusion.1 = bf16[8,576,288]{1,2,0:T(8,128)(2,1)} fusion(bf16[576,8,288]{0,2,1:T(8,128)(2,1)S(1)} %bitcast.37, s32[1024]{0:T(1024)S(1)} %pad_clamp_fusion), kind=kCustom, calls=%fused_computation.1.clone | custom fusion | bytes 5308448 | tf_op jit(solution)/shard_map/jit(_take)/gather | solution.py:65
  38.6 3.9 %select_bitcast_fusion = bf16[576,8,288]{0,2,1:T(8,128)(2,1)} fusion(bf16[8,576,288]{1,2,0:T(8,128)(2,1)} %gather_fusion.1, pred[8]{0:T(512)(128)(4,1)S(1)} %get-tuple-element.15), kind=kLoop, calls=%fused_computation.4 | loop fusion | flops 1327104 | bytes 5308424 | tf_op jit(solution)/shard_map/jit(_take)/select_n | solution.py:65
  42.4 24.4 %all-to-all-done.1 = bf16[576,8,288]{0,2,1:T(8,128)(2,1)} async-done(((bf16[576,8,288]{0,2,1:T(8,128)(2,1)}), bf16[576,8,288]{0,2,1:T(8,128)(2,1)}, u32[]{:S(2)}, u32[]{:S(2)}) %all-to-all-start.1) | async-done | bytes 2654240 | tf_op jit(solution)/shard_map/all_to_all | solution.py:81
  66.9 4.5 %all-to-all-start.3 = ((bf16[576,8,288]{0,2,1:T(8,128)(2,1)}), bf16[576,8,288]{0,2,1:T(8,128)(2,1)}, u32[]{:S(2)}, u32[]{:S(2)}) async-start(bf16[576,8,288]{0,2,1:T(8,128)(2,1)} %select_bitcast_fusion), calls=%async_computation.3 | async-start | bytes 5898240 | tf_op jit(solution)/shard_map/all_to_all | solution.py:88
  71.3 4.5 %copy.47 = bf16[8,576,288]{1,0,2:T(8,128)(2,1)} copy(bf16[8,576,288]{1,2,0:T(8,128)(2,1)} %bitcast.3) | data formatting | bytes 5308416 | tf_op jit(solution)/shard_map/all_to_all | solution.py:81
  75.8 5.4 %all_to_all.55 = bf16[16,288,288]{1,0,2:T(8,128)(2,1)S(1)} reshape(bf16[8,576,288]{1,0,2:T(8,128)(2,1)} %copy.47) | data formatting | bytes 5308416 | tf_op jit(solution)/shard_map/all_to_all | solution.py:80
  81.2 2.5 %copy.48 = bf16[16,288,288]{1,2,0:T(8,128)(2,1)} copy(bf16[16,288,288]{1,0,2:T(8,128)(2,1)S(1)} %all_to_all.55) | data formatting | bytes 5308416 | tf_op jit(solution)/shard_map/all_to_all | solution.py:80
  83.7 23.9 %all-to-all-done.3 = bf16[576,8,288]{0,2,1:T(8,128)(2,1)} async-done(((bf16[576,8,288]{0,2,1:T(8,128)(2,1)}), bf16[576,8,288]{0,2,1:T(8,128)(2,1)}, u32[]{:S(2)}, u32[]{:S(2)}) %all-to-all-start.3) | async-done | bytes 2654240 | tf_op jit(solution)/shard_map/all_to_all | solution.py:88
  107.6 8.3 %all-to-all-start.2 = ((bf16[16,288,288]{1,2,0:T(8,128)(2,1)}), bf16[16,288,288]{1,2,0:T(8,128)(2,1)S(1)}, u32[]{:S(2)}, u32[]{:S(2)}) async-start(bf16[16,288,288]{1,2,0:T(8,128)(2,1)} %copy.48), calls=%async_computation.2 | async-start | bytes 7077888 | tf_op jit(solution)/shard_map/all_to_all | solution.py:80
  115.9 4.4 %copy.51 = bf16[8,576,288]{1,0,2:T(8,128)(2,1)} copy(bf16[8,576,288]{1,2,0:T(8,128)(2,1)} %bitcast.9) | data formatting | bytes 5308416 | tf_op jit(solution)/shard_map/all_to_all | solution.py:88
  120.3 6.5 %all_to_all.61 = bf16[16,288,288]{1,0,2:T(8,128)(2,1)} reshape(bf16[8,576,288]{1,0,2:T(8,128)(2,1)} %copy.51) | data formatting | bytes 5308416 | tf_op jit(solution)/shard_map/all_to_all | solution.py:87
  126.9 4.6 %copy.52 = bf16[16,288,288]{1,2,0:T(8,128)(2,1)} copy(bf16[16,288,288]{1,0,2:T(8,128)(2,1)} %all_to_all.61) | data formatting | bytes 5308416 | tf_op jit(solution)/shard_map/all_to_all | solution.py:87
  131.4 28.8 %all-to-all-done.2 = bf16[16,288,288]{1,2,0:T(8,128)(2,1)S(1)} async-done(((bf16[16,288,288]{1,2,0:T(8,128)(2,1)}), bf16[16,288,288]{1,2,0:T(8,128)(2,1)S(1)}, u32[]{:S(2)}, u32[]{:S(2)}) %all-to-all-start.2) | async-done | bytes 2654240 | tf_op jit(solution)/shard_map/all_to_all | solution.py:80
  160.2 11.6 %all-to-all-start.4 = ((bf16[16,288,288]{1,2,0:T(8,128)(2,1)}), bf16[16,288,288]{1,2,0:T(8,128)(2,1)}, u32[]{:S(2)}, u32[]{:S(2)}) async-start(bf16[16,288,288]{1,2,0:T(8,128)(2,1)} %copy.52), calls=%async_computation.4 | async-start | bytes 7077888 | tf_op jit(solution)/shard_map/all_to_all | solution.py:87
  171.8 0.2 select_reduce_fusion
  172.0 0.6 fusion.4
  176.4 1.4 div.21
  177.8 0.7 div.19
  178.5 0.7 constant_dynamic-slice_fusion
  179.2 0.7 constant_dynamic-slice_fusion.1
  179.9 19.4 %all-gather.3 = f32[2,2,288]{2,1,0:T(2,128)S(1)} all-gather(f32[1,2,288]{2,1,0:T(2,128)S(1)} %maximum_bitcast_fusion), channel_id=2, replica_groups=mesh['row'=8,'col_0'=4,'col_1'=2,'col_2'=2] {'col_1'}, dimensions={0}, use_global_device_ids=true | all-gather | bytes 6912 | tf_op jit(solution)/shard_map/all_gather | solution.py:42
  199.3 26.1 %all-gather.1 = f32[8,2,288]{2,1,0:T(2,128)S(1)} all-gather(f32[2,2,288]{2,1,0:T(2,128)S(1)} %all-gather.3), channel_id=3, replica_groups=mesh['row'=8,'col_0'=4,'col_1'=2,'col_2'=2] {'col_0'}, dimensions={0}, use_global_device_ids=true | all-gather | bytes 23040 | tf_op jit(solution)/shard_map/all_gather | solution.py:42
  225.5 4.5 %all-gather.2 = f32[8,2,2,288]{3,2,1,0:T(2,128)S(1)} all-gather(f32[4,2,2,288]{3,2,1,0:T(2,128)S(1)} %bitcast.41), channel_id=4, replica_groups=mesh['row'=8,'col_0'=4,'col_1'=2,'col_2'=2] {'col_2'}, dimensions={0}, use_global_device_ids=true | all-gather | bytes 55296 | tf_op jit(solution)/shard_map/all_gather | solution.py:42
  230.0 0.6 copy.55
  230.6 1.5 reshape.79
  232.2 2.8 %copy.56 = bf16[288,4608]{1,0:T(8,128)(2,1)} copy(bf16[288,4608]{0,1:T(8,128)(2,1)S(1)} %bitcast.38) | data formatting | bytes 5308416 | tf_op jit(solution)/shard_map/all_to_all | solution.py:80
  235.0 0.0 all-to-all-done.4
  235.0 4.6 %copy.57 = bf16[288,4608]{1,0:T(8,128)(2,1)} copy(bf16[288,4608]{0,1:T(8,128)(2,1)} %bitcast.11) | data formatting | bytes 5308416 | tf_op jit(solution)/shard_map/all_to_all | solution.py:87
  (6 shorter events, 0.1 us)
Async XLA Ops:
  0.6 10.3 %copy-start = (bf16[576,2304]{1,0:T(8,128)(2,1)S(1)}, bf16[576,2304]{1,0:T(8,128)(2,1)}, u32[]{:S(2)}) copy-start(bf16[576,2304]{1,0:T(8,128)(2,1)} %param.5) | copy-start | bytes 7962628
  0.6 10.2 %copy-start.2 = (s32[2,8]{1,0:T(2,128)S(1)}, s32[2,8]{1,0:T(2,128)}, u32[]{:S(2)}) copy-start(s32[2,8]{1,0:T(2,128)} %param.7) | copy-start | bytes 196
  4.7 11.7 %all-to-all-start = ((f32[8,1,4608]{2,1,0:T(1,128)}), f32[8,1,4608]{2,1,0:T(1,128)S(1)}, u32[]{:S(2)}, u32[]{:S(2)}) async-start(f32[8,1,4608]{2,1,0:T(1,128)} %broadcast_in_dim.25), calls=%async_computation | async-start | bytes 294912 | tf_op jit(solution)/shard_map/all_to_all | solution.py:14
  25.9 4.7 %copy-start.1 = (bf16[576,2304]{1,0:T(8,128)(2,1)S(1)}, bf16[576,2304]{1,0:T(8,128)(2,1)}, u32[]{:S(2)}) copy-start(bf16[576,2304]{1,0:T(8,128)(2,1)} %param.6) | copy-start | bytes 7962628
  25.9 41.0 %all-to-all-start.1 = ((bf16[576,8,288]{0,2,1:T(8,128)(2,1)}), bf16[576,8,288]{0,2,1:T(8,128)(2,1)}, u32[]{:S(2)}, u32[]{:S(2)}) async-start(bf16[576,8,288]{0,2,1:T(8,128)(2,1)} %select_bitcast_fusion.1), calls=%async_computation.1 | async-start | bytes 5898240 | tf_op jit(solution)/shard_map/all_to_all | solution.py:81
  66.9 40.7 %all-to-all-start.3 = ((bf16[576,8,288]{0,2,1:T(8,128)(2,1)}), bf16[576,8,288]{0,2,1:T(8,128)(2,1)}, u32[]{:S(2)}, u32[]{:S(2)}) async-start(bf16[576,8,288]{0,2,1:T(8,128)(2,1)} %select_bitcast_fusion), calls=%async_computation.3 | async-start | bytes 5898240 | tf_op jit(solution)/shard_map/all_to_all | solution.py:88
  107.6 52.6 %all-to-all-start.2 = ((bf16[16,288,288]{1,2,0:T(8,128)(2,1)}), bf16[16,288,288]{1,2,0:T(8,128)(2,1)S(1)}, u32[]{:S(2)}, u32[]{:S(2)}) async-start(bf16[16,288,288]{1,2,0:T(8,128)(2,1)} %copy.48), calls=%async_computation.2 | async-start | bytes 7077888 | tf_op jit(solution)/shard_map/all_to_all | solution.py:80
  160.2 74.8 %all-to-all-start.4 = ((bf16[16,288,288]{1,2,0:T(8,128)(2,1)}), bf16[16,288,288]{1,2,0:T(8,128)(2,1)}, u32[]{:S(2)}, u32[]{:S(2)}) async-start(bf16[16,288,288]{1,2,0:T(8,128)(2,1)} %copy.52), calls=%async_computation.4 | async-start | bytes 7077888 | tf_op jit(solution)/shard_map/all_to_all | solution.py:87
where the time goes:
time: 241 us; the launch traced here: 240 us
  waiting for transfers between devices  79.7 us (33%)
  local copies, waits for them, and re-layouts  53.4 us (22%)
  blocking collectives  50.1 us (21%)
  starting transfers between devices  35.2 us (15%)
  other arithmetic  16.7 us (7%)
  between operations  4.63 us (2%)
    all_gather x3, blocking collectives, all_blocks(): pieces = lax.all_gather(pieces, axes[k])  50.1 us
    all_to_all x1, waiting for transfers between devices, shards(): lax.all_to_all(lax.all_to_all(gate_sent, 'row', split_axis=1, concat_axis...  28.8 us
    all_to_all x1, waiting for transfers between devices, shards(): lax.all_to_all(gate_sent, 'row', split_axis=1, concat_axis=0, tiled=True)  24.4 us
    all_to_all x1, waiting for transfers between devices, shards(): lax.all_to_all(up_sent, 'row', split_axis=1, concat_axis=0, tiled=True)  23.9 us
    all_to_all x3, local copies, waits for them, and re-layouts, shards(): lax.all_to_all(lax.all_to_all(up_sent, 'row', split_axis=1, concat_axis=0...  15.8 us
    all_to_all x1, starting transfers between devices, shards(): lax.all_to_all(lax.all_to_all(up_sent, 'row', split_axis=1, concat_axis=0...  11.6 us
    all_to_all x3, local copies, waits for them, and re-layouts, shards(): lax.all_to_all(lax.all_to_all(gate_sent, 'row', split_axis=1, concat_axis...  10.7 us
    all_to_all x1, starting transfers between devices, shards(): lax.all_to_all(lax.all_to_all(gate_sent, 'row', split_axis=1, concat_axis...  8.29 us
  transfers between devices with their start and end apart: 5, of which 4 were waited for; matrix products, arithmetic and copies ran while one was open for 17% of the time, Pallas kernels for 0%

commit v1 on v0

--- a/solution.py
+++ b/solution.py
@@ -1,3 +1,4 @@
+import functools
 import jax
 import jax.numpy as jnp
 from jax import lax
@@ -7,6 +8,22 @@
 COL = ("col_0", "col_1", "col_2")
 EPSILON = 1e-06
 LIMIT = 4.0
+
+
+def guide_the_types(local_block, axis_key):
+    view_out = jnp.concatenate(
+        jax.lax.all_to_all(
+            jnp.stack(jnp.split(local_block, jax.lax.axis_size(axis_key), axis=0)),
+            axis_key,
+            concat_axis=0,
+            split_axis=0,
+        ),
+        axis=1,
+    )
+    return view_out
+
+
+_get_cubes = functools.partial(guide_the_types, axis_key=COL)
 
 
 def copy_for_each(value, axis):
@@ -77,13 +94,7 @@
     gate_sent = order_pieces(quantize(gate_weight, gate_peaks), routes[0], pieces)
     up_sent = order_pieces(quantize(up_weight, up_peaks), routes[1], pieces)
     gate_serving, up_serving = (
-        lax.all_to_all(
-            lax.all_to_all(gate_sent, "row", split_axis=1, concat_axis=0, tiled=True),
-            COL,
-            split_axis=0,
-            concat_axis=1,
-            tiled=True,
-        ),
+        _get_cubes(lax.all_to_all(gate_sent, "row", split_axis=1, concat_axis=0, tiled=True)),
         lax.all_to_all(
             lax.all_to_all(up_sent, "row", split_axis=1, concat_axis=0, tiled=True),
             COL,

time: 241 us -> 241 us (level)
  waiting for transfers between devices: 79.7 us -> 70.2 us
  local copies, waits for them, and re-layouts: 53.4 us -> 62.7 us
    unnamed x8 -> x23, local copies, waits for them, and re-layouts: 5.95 us -> 17.8 us
    all_to_all x3 -> x0, local copies, waits for them, and re-layouts: 10.7 us -> none  [shards(): lax.all_to_all(lax.all_to_all(gate_sent, 'row', split_axis=1, concat_axis...]
    all_to_all x1, waiting for transfers between devices: 23.9 us -> 14.5 us  [shards(): lax.all_to_all(up_sent, 'row', split_axis=1, concat_axis=0, tiled=True)]
    all_to_all x1 -> x2, local copies, waits for them, and re-layouts: 4.46 us -> 9 us  [shards(): lax.all_to_all(gate_sent, 'row', split_axis=1, concat_axis=0, tiled=True)]
    reshape x0 -> x1, local copies, waits for them, and re-layouts: none -> 2.82 us  [guide_the_types(): jnp.concatenate(jax.lax.all_to_all(jnp.stack(jnp.split(local_block, jax.l...]
  transfers between devices with their start and end apart: 5 -> 5, of which waited for: 4 -> 4; matrix products, arithmetic and copies ran while one was open for 17% -> 21% of each run, Pallas kernels for 0% -> 0%
where the time goes in v1:
time: 241 us; the launch traced here: 240 us
  waiting for transfers between devices  70.2 us (29%)
  local copies, waits for them, and re-layouts  62.7 us (26%)
  blocking collectives  50.1 us (21%)
  starting transfers between devices  35.2 us (15%)
  other arithmetic  16.7 us (7%)
  between operations  4.64 us (2%)
    all_gather x3, blocking collectives, all_blocks(): pieces = lax.all_gather(pieces, axes[k])  50.1 us
    all_to_all x1, waiting for transfers between devices, guide_the_types(): jax.lax.all_to_all(jnp.stack(jnp.split(local_block, jax.lax.axis_size(axi...  28.8 us
    all_to_all x1, waiting for transfers between devices, shards(): lax.all_to_all(gate_sent, 'row', split_axis=1, concat_axis=0, tiled=True)  24.4 us
    unnamed x23, local copies, waits for them, and re-layouts  17.8 us
    all_to_all x3, local copies, waits for them, and re-layouts, shards(): lax.all_to_all(lax.all_to_all(up_sent, 'row', split_axis=1, concat_axis=0...  15.7 us
    all_to_all x1, waiting for transfers between devices, shards(): lax.all_to_all(up_sent, 'row', split_axis=1, concat_axis=0, tiled=True)  14.5 us
    all_to_all x1, starting transfers between devices, shards(): lax.all_to_all(lax.all_to_all(up_sent, 'row', split_axis=1, concat_axis=0...  11.6 us
    all_to_all x2, local copies, waits for them, and re-layouts, shards(): lax.all_to_all(gate_sent, 'row', split_axis=1, concat_axis=0, tiled=True)  9 us
  transfers between devices with their start and end apart: 5, of which 4 were waited for; matrix products, arithmetic and copies ran while one was open for 21% of the time, Pallas kernels for 0%

profile of v1, /device:TPU:1, one launch (start us, length us, event | category | flops | bytes accessed | tf_op | source)
XLA Modules:
  0.0 239.5 jit_solution(4610531223259248276)
XLA Ops:
  0.6 0.0 copy-start
  0.6 0.0 copy-start.2
  0.7 3.3 %abs_reduce_fusion = (bf16[2304]{0:T(1024)(128)(2,1)S(1)}, bf16[2304]{0:T(1024)(128)(2,1)S(1)}) fusion(bf16[576,2304]{1,0:T(8,128)(2,1)} %param.6, bf16[576,2304]{1,0:T(8,128)(2,1)} %param.5), kind=kLoop, calls=%fused_computation.6 | loop fusion | flops 5303808 | bytes 5317632 | tf_op jit(solution)/shard_map/reduce_max | solution.py:71
  3.9 0.7 broadcast_in_dim.25
  4.7 6.2 %all-to-all-start = ((f32[8,1,4608]{2,1,0:T(1,128)}), f32[8,1,4608]{2,1,0:T(1,128)S(1)}, u32[]{:S(2)}, u32[]{:S(2)}) async-start(f32[8,1,4608]{2,1,0:T(1,128)} %broadcast_in_dim.25), calls=%async_computation | async-start | bytes 294912 | tf_op jit(solution)/shard_map/all_to_all | solution.py:31
  10.9 0.0 copy-done.2
  10.9 0.0 copy-done
  10.9 3.0 %copy.66 = bf16[576,2304]{0,1:T(8,128)(2,1)} copy(bf16[576,2304]{1,0:T(8,128)(2,1)S(1)} %copy-done) | data formatting | bytes 5308416 | tf_op args[0]
  13.9 2.5 %all-to-all-done = f32[8,1,4608]{2,1,0:T(1,128)S(1)} async-done(((f32[8,1,4608]{2,1,0:T(1,128)}), f32[8,1,4608]{2,1,0:T(1,128)S(1)}, u32[]{:S(2)}, u32[]{:S(2)}) %all-to-all-start) | async-done | bytes 147488 | tf_op jit(solution)/shard_map/all_to_all | solution.py:31
  16.4 0.1 reduce_max.29
  16.5 0.6 fusion.16
  17.1 2.4 multiply_convert_fusion.1
  19.5 2.5 %gather_fusion = bf16[8,576,288]{1,2,0:T(8,128)(2,1)} fusion(bf16[576,8,288]{0,2,1:T(8,128)(2,1)S(1)} %bitcast.100, s32[1024]{0:T(1024)S(1)} %pad_clamp_fusion.1), kind=kCustom, calls=%fused_computation.clone | custom fusion | bytes 5308448 | tf_op jit(solution)/shard_map/jit(_take)/gather | solution.py:82
  22.0 3.8 %select_bitcast_fusion.1 = bf16[576,8,288]{0,2,1:T(8,128)(2,1)} fusion(bf16[8,576,288]{1,2,0:T(8,128)(2,1)} %gather_fusion, pred[8]{0:T(512)(128)(4,1)S(1)} %get-tuple-element.23), kind=kLoop, calls=%fused_computation.5 | loop fusion | flops 1327104 | bytes 5308424 | tf_op jit(solution)/shard_map/jit(_take)/select_n | solution.py:82
  25.8 0.0 copy-start.1
  25.8 4.7 %all-to-all-start.1 = ((bf16[576,8,288]{0,2,1:T(8,128)(2,1)}), bf16[576,8,288]{0,2,1:T(8,128)(2,1)}, u32[]{:S(2)}, u32[]{:S(2)}) async-start(bf16[576,8,288]{0,2,1:T(8,128)(2,1)} %select_bitcast_fusion.1), calls=%async_computation.1 | async-start | bytes 5898240 | tf_op jit(solution)/shard_map/all_to_all | solution.py:97
  30.6 0.0 copy-done.1
  30.6 3.0 %copy.72 = bf16[576,2304]{0,1:T(8,128)(2,1)} copy(bf16[576,2304]{1,0:T(8,128)(2,1)S(1)} %copy-done.1) | data formatting | bytes 5308416 | tf_op args[1]
  33.6 2.4 multiply_convert_fusion
  36.0 2.6 %gather_fusion.1 = bf16[8,576,288]{1,2,0:T(8,128)(2,1)} fusion(bf16[576,8,288]{0,2,1:T(8,128)(2,1)S(1)} %bitcast.101, s32[1024]{0:T(1024)S(1)} %pad_clamp_fusion), kind=kCustom, calls=%fused_computation.1.clone | custom fusion | bytes 5308448 | tf_op jit(solution)/shard_map/jit(_take)/gather | solution.py:82
  38.5 3.9 %select_bitcast_fusion = bf16[576,8,288]{0,2,1:T(8,128)(2,1)} fusion(bf16[8,576,288]{1,2,0:T(8,128)(2,1)} %gather_fusion.1, pred[8]{0:T(512)(128)(4,1)S(1)} %get-tuple-element.15), kind=kLoop, calls=%fused_computation.4 | loop fusion | flops 1327104 | bytes 5308424 | tf_op jit(solution)/shard_map/jit(_take)/select_n | solution.py:82
  42.4 24.4 %all-to-all-done.1 = bf16[576,8,288]{0,2,1:T(8,128)(2,1)} async-done(((bf16[576,8,288]{0,2,1:T(8,128)(2,1)}), bf16[576,8,288]{0,2,1:T(8,128)(2,1)}, u32[]{:S(2)}, u32[]{:S(2)}) %all-to-all-start.1) | async-done | bytes 2654240 | tf_op jit(solution)/shard_map/all_to_all | solution.py:97
  66.8 4.4 %all-to-all-start.3 = ((bf16[576,8,288]{0,2,1:T(8,128)(2,1)}), bf16[576,8,288]{0,2,1:T(8,128)(2,1)}, u32[]{:S(2)}, u32[]{:S(2)}) async-start(bf16[576,8,288]{0,2,1:T(8,128)(2,1)} %select_bitcast_fusion), calls=%async_computation.3 | async-start | bytes 5898240 | tf_op jit(solution)/shard_map/all_to_all | solution.py:99
  71.3 4.5 %copy.68 = bf16[8,576,288]{1,0,2:T(8,128)(2,1)} copy(bf16[8,576,288]{1,2,0:T(8,128)(2,1)} %bitcast.3) | data formatting | bytes 5308416 | tf_op jit(solution)/shard_map/all_to_all | solution.py:97
  75.7 4.5 %all_to_all.46 = bf16[4608,288]{0,1:T(8,128)(2,1)S(1)} reshape(bf16[8,576,288]{1,0,2:T(8,128)(2,1)} %copy.68) | data formatting | bytes 5308416 | tf_op jit(solution)/shard_map/all_to_all | solution.py:97
  80.3 0.7 fusion.15
  81.0 0.8 fusion.14
  81.8 0.8 fusion.13
  82.6 0.8 fusion.12
  83.4 0.7 fusion.11
  84.1 0.9 fusion.10
  85.0 0.8 fusion.9
  85.8 0.8 fusion.8
  86.6 0.7 fusion.7
  87.4 0.8 fusion.6
  88.2 0.8 fusion.5
  89.0 0.8 fusion.4
  89.8 0.7 fusion.3
  90.5 0.8 fusion.2
  91.3 0.8 fusion.1
  92.1 0.8 fusion
  93.0 14.5 %all-to-all-done.3 = bf16[576,8,288]{0,2,1:T(8,128)(2,1)} async-done(((bf16[576,8,288]{0,2,1:T(8,128)(2,1)}), bf16[576,8,288]{0,2,1:T(8,128)(2,1)}, u32[]{:S(2)}, u32[]{:S(2)}) %all-to-all-start.3) | async-done | bytes 2654240 | tf_op jit(solution)/shard_map/all_to_all | solution.py:99
  107.5 8.3 %all-to-all-start.2 = ((bf16[16,288,288]{1,2,0:T(8,128)(2,1)}), bf16[16,288,288]{1,2,0:T(8,128)(2,1)S(1)}, u32[]{:S(2)}, u32[]{:S(2)}) async-start(bf16[16,288,288]{1,2,0:T(8,128)(2,1)} %fusion), calls=%async_computation.2 | async-start | bytes 7077888 | tf_op jit(solution)/shard_map/all_to_all | solution.py:15
  115.8 4.5 %copy.73 = bf16[8,576,288]{1,0,2:T(8,128)(2,1)} copy(bf16[8,576,288]{1,2,0:T(8,128)(2,1)} %bitcast.25) | data formatting | bytes 5308416 | tf_op jit(solution)/shard_map/all_to_all | solution.py:99
  120.3 6.5 %all_to_all.50 = bf16[16,288,288]{1,0,2:T(8,128)(2,1)} reshape(bf16[8,576,288]{1,0,2:T(8,128)(2,1)} %copy.73) | data formatting | bytes 5308416 | tf_op jit(solution)/shard_map/all_to_all | solution.py:98
  126.8 4.5 %copy.74 = bf16[16,288,288]{1,2,0:T(8,128)(2,1)} copy(bf16[16,288,288]{1,0,2:T(8,128)(2,1)} %all_to_all.50) | data formatting | bytes 5308416 | tf_op jit(solution)/shard_map/all_to_all | solution.py:98
  131.3 28.8 %all-to-all-done.2 = bf16[16,288,288]{1,2,0:T(8,128)(2,1)S(1)} async-done(((bf16[16,288,288]{1,2,0:T(8,128)(2,1)}), bf16[16,288,288]{1,2,0:T(8,128)(2,1)S(1)}, u32[]{:S(2)}, u32[]{:S(2)}) %all-to-all-start.2) | async-done | bytes 2654240 | tf_op jit(solution)/shard_map/all_to_all | solution.py:15
  160.1 11.6 %all-to-all-start.4 = ((bf16[16,288,288]{1,2,0:T(8,128)(2,1)}), bf16[16,288,288]{1,2,0:T(8,128)(2,1)}, u32[]{:S(2)}, u32[]{:S(2)}) async-start(bf16[16,288,288]{1,2,0:T(8,128)(2,1)} %copy.74), calls=%async_computation.4 | async-start | bytes 7077888 | tf_op jit(solution)/shard_map/all_to_all | solution.py:98
  171.7 0.2 select_reduce_fusion
  171.9 0.6 fusion.20
  176.4 1.4 div.21
  177.7 0.7 div.19
  178.4 0.7 constant_dynamic-slice_fusion
  179.1 0.7 constant_dynamic-slice_fusion.1
  179.8 19.4 %all-gather.3 = f32[2,2,288]{2,1,0:T(2,128)S(1)} all-gather(f32[1,2,288]{2,1,0:T(2,128)S(1)} %maximum_bitcast_fusion), channel_id=2, replica_groups=mesh['row'=8,'col_0'=4,'col_1'=2,'col_2'=2] {'col_1'}, dimensions={0}, use_global_device_ids=true | all-gather | bytes 6912 | tf_op jit(solution)/shard_map/all_gather | solution.py:59
  199.2 26.1 %all-gather.1 = f32[8,2,288]{2,1,0:T(2,128)S(1)} all-gather(f32[2,2,288]{2,1,0:T(2,128)S(1)} %all-gather.3), channel_id=3, replica_groups=mesh['row'=8,'col_0'=4,'col_1'=2,'col_2'=2] {'col_0'}, dimensions={0}, use_global_device_ids=true | all-gather | bytes 23040 | tf_op jit(solution)/shard_map/all_gather | solution.py:59
  225.4 4.5 %all-gather.2 = f32[8,2,2,288]{3,2,1,0:T(2,128)S(1)} all-gather(f32[4,2,2,288]{3,2,1,0:T(2,128)S(1)} %bitcast.105), channel_id=4, replica_groups=mesh['row'=8,'col_0'=4,'col_1'=2,'col_2'=2] {'col_2'}, dimensions={0}, use_global_device_ids=true | all-gather | bytes 55296 | tf_op jit(solution)/shard_map/all_gather | solution.py:59
  229.9 0.6 copy.77
  230.5 1.5 reshape.83
  232.1 2.8 %copy.79 = bf16[288,4608]{1,0:T(8,128)(2,1)} copy(bf16[288,4608]{0,1:T(8,128)(2,1)S(1)} %bitcast.102) | data formatting | bytes 5308416 | tf_op jit(solution)/shard_map/reshape | solution.py:14
  234.9 0.0 all-to-all-done.4
  234.9 4.6 %copy.80 = bf16[288,4608]{1,0:T(8,128)(2,1)} copy(bf16[288,4608]{0,1:T(8,128)(2,1)} %bitcast.27) | data formatting | bytes 5308416 | tf_op jit(solution)/shard_map/all_to_all | solution.py:98
  (6 shorter events, 0.1 us)
Async XLA Ops:
  0.6 10.3 %copy-start = (bf16[576,2304]{1,0:T(8,128)(2,1)S(1)}, bf16[576,2304]{1,0:T(8,128)(2,1)}, u32[]{:S(2)}) copy-start(bf16[576,2304]{1,0:T(8,128)(2,1)} %param.5) | copy-start | bytes 7962628
  0.6 10.2 %copy-start.2 = (s32[2,8]{1,0:T(2,128)S(1)}, s32[2,8]{1,0:T(2,128)}, u32[]{:S(2)}) copy-start(s32[2,8]{1,0:T(2,128)} %param.7) | copy-start | bytes 196
  4.7 11.7 %all-to-all-start = ((f32[8,1,4608]{2,1,0:T(1,128)}), f32[8,1,4608]{2,1,0:T(1,128)S(1)}, u32[]{:S(2)}, u32[]{:S(2)}) async-start(f32[8,1,4608]{2,1,0:T(1,128)} %broadcast_in_dim.25), calls=%async_computation | async-start | bytes 294912 | tf_op jit(solution)/shard_map/all_to_all | solution.py:31
  25.8 4.7 %copy-start.1 = (bf16[576,2304]{1,0:T(8,128)(2,1)S(1)}, bf16[576,2304]{1,0:T(8,128)(2,1)}, u32[]{:S(2)}) copy-start(bf16[576,2304]{1,0:T(8,128)(2,1)} %param.6) | copy-start | bytes 7962628
  25.8 41.0 %all-to-all-start.1 = ((bf16[576,8,288]{0,2,1:T(8,128)(2,1)}), bf16[576,8,288]{0,2,1:T(8,128)(2,1)}, u32[]{:S(2)}, u32[]{:S(2)}) async-start(bf16[576,8,288]{0,2,1:T(8,128)(2,1)} %select_bitcast_fusion.1), calls=%async_computation.1 | async-start | bytes 5898240 | tf_op jit(solution)/shard_map/all_to_all | solution.py:97
  66.8 40.7 %all-to-all-start.3 = ((bf16[576,8,288]{0,2,1:T(8,128)(2,1)}), bf16[576,8,288]{0,2,1:T(8,128)(2,1)}, u32[]{:S(2)}, u32[]{:S(2)}) async-start(bf16[576,8,288]{0,2,1:T(8,128)(2,1)} %select_bitcast_fusion), calls=%async_computation.3 | async-start | bytes 5898240 | tf_op jit(solution)/shard_map/all_to_all | solution.py:99
  107.5 52.6 %all-to-all-start.2 = ((bf16[16,288,288]{1,2,0:T(8,128)(2,1)}), bf16[16,288,288]{1,2,0:T(8,128)(2,1)S(1)}, u32[]{:S(2)}, u32[]{:S(2)}) async-start(bf16[16,288,288]{1,2,0:T(8,128)(2,1)} %fusion), calls=%async_computation.2 | async-start | bytes 7077888 | tf_op jit(solution)/shard_map/all_to_all | solution.py:15
  160.1 74.8 %all-to-all-start.4 = ((bf16[16,288,288]{1,2,0:T(8,128)(2,1)}), bf16[16,288,288]{1,2,0:T(8,128)(2,1)}, u32[]{:S(2)}, u32[]{:S(2)}) async-start(bf16[16,288,288]{1,2,0:T(8,128)(2,1)} %copy.74), calls=%async_computation.4 | async-start | bytes 7077888 | tf_op jit(solution)/shard_map/all_to_all | solution.py:98
